TPU v7x, 32 devices: a whole 2x2x4 slice. The times are simulated.
32 devices in a mesh: leaf: 4 (over y, core), grid: 8 (over z, x).
Axes of the slice: x: 2, y: 2, z: 4, core: 2. Of those that a mesh axis runs over, the one named last changes fastest.
Arguments:
- ainv_sep: bfloat16 [4, 2048, 2048], P('leaf', 'grid'), may hold values from -6 to 6
- l_panel: bfloat16 [4, 2048, 512], P('leaf', 'grid'), may hold values from -0.125 to 0.125
- block_mask: int32 [4, 1, 4], P('leaf'), may hold values 0 or 1
- owner: int32 [4, 4], P('leaf'), may hold values 0 or 1
- dinv: float32 [4, 512, 512], P('leaf', 'grid'), may hold values from -6 to 6
Outputs:
- ainv_panel: bfloat16 [4, 2048, 512], P('leaf', 'grid')
- ainv_upper: bfloat16 [4, 512, 2048], P('leaf', 'grid')
- ainv_diag: float32 [4, 512, 512], P('leaf', 'grid')
All inputs are finite; a program needn't handle non-finite values. No bound on the sum of `block_mask` or of `owner` on one device may be relied on, other than what follows from the above.
Results may differ from a plain program's by a relative error of at most 0.0019.
Values may be sent and summed in bfloat16 or wider, within the bound.
No kernel may reach another device: no remote copies, remote signals or barrier semaphores. Data moves between devices by JAX's collectives and lax.ppermute only.
A program may use at most 128 MiB of HBM per device.

v0:
```python
import jax
import jax.numpy as jnp
from jax import lax
from jax.sharding import PartitionSpec as P

B = 512


def swapped(array, axis, stride):
    return lax.ppermute(array, axis, [(i, i ^ 1 << stride) for i in range(lax.axis_size(axis))])


def body(ainv_sep, l_panel, block_mask, owner, dinv):
    strip_rows = ainv_sep.shape[1]
    block_count = block_mask.shape[2]
    sibling = swapped(ainv_sep, "leaf", 0)
    colmask = jnp.repeat(owner[0], B)
    mixed = jnp.where(colmask[None, :] == 1, sibling[0], ainv_sep[0])
    first_row = lax.axis_index("grid") * strip_rows
    row_block = (first_row + jnp.arange(strip_rows, dtype=jnp.int32)) // B
    onehot = (row_block[:, None] == jnp.arange(block_count, dtype=jnp.int32)[None, :]).astype(
        jnp.float32
    )
    row_flags = jnp.dot(
        onehot, block_mask[0].T.astype(jnp.float32), preferred_element_type=jnp.float32
    )
    flags_wide = jnp.repeat(row_flags, B, axis=1)
    masked = jnp.where(flags_wide > 0.5, l_panel[0], jnp.zeros((), jnp.bfloat16))
    whole_panel = lax.all_gather(masked, "grid", axis=0, tiled=True)
    panel = (-jnp.dot(mixed, whole_panel, preferred_element_type=jnp.float32)).astype(jnp.bfloat16)
    upper = lax.all_to_all(panel.T, "grid", split_axis=0, concat_axis=1, tiled=True)
    diag = dinv[0] - jnp.dot(upper, whole_panel, preferred_element_type=jnp.float32)
    return (panel[None], upper[None], diag[None])


def solution(mesh):
    placed = (
        P("leaf", "grid", None),
        P("leaf", "grid", None),
        P("leaf", None, None),
        P("leaf", None),
        P("leaf", "grid", None),
    )
    return jax.shard_map(
        body,
        mesh=mesh,
        in_specs=placed,
        out_specs=(P("leaf", "grid", None), P("leaf", "grid", None), P("leaf", "grid", None)),
        check_vma=False,
    )
```

profile of v0, /device:TPU:0, one launch (start us, length us, event | category | flops | bytes accessed | tf_op | source)
XLA Modules:
  0.0 85.9 jit_solution(1391319304822525056)
XLA Ops:
  7.2 0.0 all-gather.2.cloned.1.call-start
  7.2 0.9 %fusion.4 = f32[1,256]{1,0:T(1,128)S(1)} fusion(s32[256]{0:T(256)S(1)} %and_select_fusion, s32[1,1,4]{2,1,0:T(1,128)} %param.7), kind=kOutput, calls=%fused_computation.9 | convolution fusion | flops 3076 | bytes 2064 | tf_op jit(solution)/shard_map/dot_general | solution.py:24
  8.1 1.8 %bitcast_select_fusion.2 = bf16[256,512]{1,0:T(8,128)(2,1)} fusion(bf16[1,256,512]{2,1,0:T(8,128)(2,1)} %param.6, pred[256]{0:T(512)(128)(4,1)S(1)} %broadcast_compare_fusion), kind=kLoop, calls=%fused_computation.7 | loop fusion | flops 131072 | bytes 524544 | tf_op jit(solution)/shard_map/jit(_where)/select_n | solution.py:28
  9.9 0.0 all-gather.2.cloned.1.call-update
  9.9 0.6 collective-permute-start
  10.5 0.7 compare_bitcast_fusion
  11.1 0.1 broadcast_bitcast_fusion
  11.2 1.8 %collective-permute-done = bf16[1,256,2048]{2,1,0:T(8,128)(2,1)S(1)} collective-permute-done((bf16[1,256,2048]{2,1,0:T(8,128)(2,1)}, bf16[1,256,2048]{2,1,0:T(8,128)(2,1)S(1)}, u32[]{:S(2)}, u32[]{:S(2)}) %collective-permute-start) | collective-permute-done | bytes 1048608 | tf_op jit(solution)/shard_map/ppermute | solution.py:10
  13.0 49.6 %all-gather.2.cloned.1.call-done = bf16[2048,512]{1,0:T(8,128)(2,1)} async-done(((bf16[256,512]{1,0:T(8,128)(2,1)}), bf16[2048,512]{1,0:T(8,128)(2,1)}) %all-gather.2.cloned.1.call-update) | async-done | bytes 2097168 | tf_op jit(solution)/shard_map/all_gather | solution.py:29
  62.5 2.7 %fusion = bf16[256,512]{1,0:T(8,128)(2,1)S(1)} fusion(bf16[2048,512]{1,0:T(8,128)(2,1)} %all-gather.2.cloned.1.call-done, bf16[1,256,2048]{2,1,0:T(8,128)(2,1)} %param.5, bf16[1,256,2048]{2,1,0:T(8,128)(2,1)S(1)} %collective-permute-done, pred[2048]{0:T(1024)(128)(4,1)S(1)} %bitcast.40), kind=kOutput, calls=%fused_computation.1 | convolution fusion | flops 537657344 | bytes 4458496 | tf_op jit(solution)/shard_map/dot_general | solution.py:30
  65.2 0.0 copy-start.1
  65.2 0.0 copy-start
  65.2 0.0 copy-start.2
  65.2 0.1 copy.11
  65.4 11.6 %all_to_all.19 = bf16[8,64,256]{2,1,0:T(8,128)(2,1)S(1)} all-to-all(bf16[8,64,256]{2,1,0:T(8,128)(2,1)S(1)} %bitcast.37), channel_id=1, replica_groups=mesh['leaf'=4,'grid'=8] {'grid'}, dimensions={0} | all-to-all | bytes 524288 | tf_op jit(solution)/shard_map/all_to_all | solution.py:31
  76.9 0.1 copy.12
  77.1 0.8 broadcast_in_dim.31
  77.9 0.0 copy-done
  77.9 0.0 copy-done.2
  77.9 1.1 %fusion.1 = f32[1,64,512]{2,1,0:T(8,128)} fusion(bf16[64,2048]{1,0:T(8,128)(2,1)S(1)} %bitcast.36, bf16[2048,512]{1,0:T(8,128)(2,1)S(1)} %copy-done, f32[1,64,512]{2,1,0:T(8,128)S(1)} %copy-done.2), kind=kOutput, calls=%fused_computation.3 | convolution fusion | flops 134250496 | bytes 2621440 | tf_op jit(solution)/shard_map/dot_general | solution.py:32
  79.1 0.0 copy-done.1
  (4 shorter events, 0.0 us)
Async XLA Ops:
  7.2 55.3 %all-gather.2.cloned.1.call-start = ((), (), s32[]{:S(2)}) async-start(), calls=%async_computation.1 | async-start | bytes 2359296 | tf_op jit(solution)/shard_map/all_gather | solution.py:29
  9.9 3.1 %collective-permute-start = (bf16[1,256,2048]{2,1,0:T(8,128)(2,1)}, bf16[1,256,2048]{2,1,0:T(8,128)(2,1)S(1)}, u32[]{:S(2)}, u32[]{:S(2)}) collective-permute-start(bf16[1,256,2048]{2,1,0:T(8,128)(2,1)} %param.5), channel_id=1, source_target_pairs={{0,8},{8,0},{16,24},{24,16},{1,9},{9,1},{17,25},{25,17},{2,10},{10... | collective-permute-start | bytes 3145736 | tf_op jit(solution)/shard_map/ppermute | solution.py:10
  65.2 13.9 %copy-start.1 = (bf16[256,512]{1,0:T(8,128)(2,1)}, bf16[256,512]{1,0:T(8,128)(2,1)S(1)}, u32[]{:S(2)}) copy-start(bf16[256,512]{1,0:T(8,128)(2,1)S(1)} %fusion) | copy-start | bytes 786436
  65.2 12.7 %copy-start = (bf16[2048,512]{1,0:T(8,128)(2,1)S(1)}, bf16[2048,512]{1,0:T(8,128)(2,1)}, u32[]{:S(2)}) copy-start(bf16[2048,512]{1,0:T(8,128)(2,1)} %all-gather.2.cloned.1.call-done) | copy-start | bytes 6291460
  65.2 12.7 %copy-start.2 = (f32[1,64,512]{2,1,0:T(8,128)S(1)}, f32[1,64,512]{2,1,0:T(8,128)}, u32[]{:S(2)}) copy-start(f32[1,64,512]{2,1,0:T(8,128)} %param.9) | copy-start | bytes 393220
Sparse Core Ops, SparseCore 0:
  10.7 51.7 all-gather.1
where the time goes:
time: 86.2 us; the launch traced here: 85.9 us
  waiting for transfers between devices  51.3 us (60%)
  between operations  14.1 us (16%)
  blocking collectives  11.6 us (13%)
  matrix products  4.67 us (5%)
  other arithmetic  2.44 us (3%)
  local copies, waits for them, and re-layouts  1.23 us (1%)
    all_gather x1, waiting for transfers between devices, body(): whole_panel = lax.all_gather(masked, 'grid', axis=0, tiled=True)  49.6 us
    all_to_all x1, blocking collectives, body(): lax.all_to_all(panel.T, 'grid', split_axis=0, concat_axis=1, tiled=True)  11.6 us
    dot_general x1, matrix products, body(): jnp.dot(mixed, whole_panel, preferred_element_type=jnp.float32)  2.66 us
    select_n x1, other arithmetic, body(): jnp.where(flags_wide > 0.5, l_panel[0], jnp.zeros((), jnp.bfloat16))  1.76 us
    ppermute x1, waiting for transfers between devices, swapped(): lax.ppermute(array, axis, [(i, i ^ 1 << stride) for i in range(lax.axis_s...  1.75 us
  transfers between devices with their start and end apart: 2, of which 2 were waited for; matrix products, arithmetic and copies ran while one was open for 1% of the time, Pallas kernels for 0%

commit v1 on v0

--- a/solution.py
+++ b/solution.py
@@ -26,7 +26,16 @@
     )
     flags_wide = jnp.repeat(row_flags, B, axis=1)
     masked = jnp.where(flags_wide > 0.5, l_panel[0], jnp.zeros((), jnp.bfloat16))
-    whole_panel = lax.all_gather(masked, "grid", axis=0, tiled=True)
+    axis_n = lax.psum(1, axis_name="grid")
+    extra = sorted(((hop_no, (hop_no + 1) % axis_n) for hop_no in range(axis_n)))
+    plain = masked
+    pages = [plain]
+    for rr in range(1, axis_n):
+        plain = lax.ppermute(plain, "grid", extra)
+        pages.insert(0, plain)
+    s_next = jnp.concatenate(pages, axis=0)
+    arr_now = lax.axis_index("grid") + 1
+    whole_panel = jnp.roll(s_next, arr_now * masked.shape[0], axis=0)
     panel = (-jnp.dot(mixed, whole_panel, preferred_element_type=jnp.float32)).astype(jnp.bfloat16)
     upper = lax.all_to_all(panel.T, "grid", split_axis=0, concat_axis=1, tiled=True)
     diag = dinv[0] - jnp.dot(upper, whole_panel, preferred_element_type=jnp.float32)

time: 86.2 us -> 89.5 us (1.038)
  waiting for transfers between devices: 51.3 us -> 64.9 us
  between operations: 14.1 us -> 0.86 us
  starting transfers between devices: 0.6 us -> 3.04 us
  local copies, waits for them, and re-layouts: 1.23 us -> 3.44 us
  blocking collectives: 11.6 us -> 10.6 us
    ppermute x0 -> x7, waiting for transfers between devices: none -> 64.9 us  [body(): plain = lax.ppermute(plain, 'grid', extra)]
    all_gather x1 -> x0, waiting for transfers between devices: 49.6 us -> none  [body(): whole_panel = lax.all_gather(masked, 'grid', axis=0, tiled=True)]
    ppermute x0 -> x7, starting transfers between devices: none -> 3.04 us  [body(): plain = lax.ppermute(plain, 'grid', extra)]
    unnamed x8 -> x26, local copies, waits for them, and re-layouts: 0.1 us -> 2.31 us
    dot_general x1, matrix products: 2.66 us -> 0.74 us  [body(): jnp.dot(mixed, whole_panel, preferred_element_type=jnp.float32)]
    ppermute x1, waiting for transfers between devices: 1.75 us -> 0.01 us  [swapped(): lax.ppermute(array, axis, [(i, i ^ 1 << stride) for i in range(lax.axis_s...]
    dot_general x1, matrix products: 1.13 us -> 2.72 us  [body(): jnp.dot(upper, whole_panel, preferred_element_type=jnp.float32)]
    all_to_all x1, blocking collectives: 11.6 us -> 10.6 us  [body(): lax.all_to_all(panel.T, 'grid', split_axis=0, concat_axis=1, tiled=True)]
  transfers between devices with their start and end apart: 2 -> 8, of which waited for: 2 -> 7; matrix products, arithmetic and copies ran while one was open for 1% -> 1% of each run, Pallas kernels for 0% -> 0%
where the time goes in v1:
time: 89.5 us; the launch traced here: 89.2 us
  waiting for transfers between devices  64.9 us (73%)
  blocking collectives  10.6 us (12%)
  matrix products  4.37 us (5%)
  local copies, waits for them, and re-layouts  3.44 us (4%)
  starting transfers between devices  3.04 us (3%)
  other arithmetic  1.96 us (2%)
    ppermute x7, waiting for transfers between devices, body(): plain = lax.ppermute(plain, 'grid', extra)  64.9 us
    all_to_all x1, blocking collectives, body(): lax.all_to_all(panel.T, 'grid', split_axis=0, concat_axis=1, tiled=True)  10.6 us
    ppermute x7, starting transfers between devices, body(): plain = lax.ppermute(plain, 'grid', extra)  3.04 us
    dot_general x1, matrix products, body(): jnp.dot(upper, whole_panel, preferred_element_type=jnp.float32)  2.72 us
    unnamed x26, local copies, waits for them, and re-layouts  2.31 us
  transfers between devices with their start and end apart: 8, of which 7 were waited for; matrix products, arithmetic and copies ran while one was open for 1% of the time, Pallas kernels for 0%

profile of v1, /device:TPU:0, one launch (start us, length us, event | category | flops | bytes accessed | tf_op | source)
XLA Modules:
  0.0 89.2 jit_solution(5227503015086629828)
XLA Ops:
  0.6 0.0 copy-start
  0.7 0.9 %fusion.18 = f32[1,256]{1,0:T(1,128)S(1)} fusion(s32[256]{0:T(256)S(1)} %and_select_fusion, s32[1,1,4]{2,1,0:T(1,128)} %param.7), kind=kOutput, calls=%fused_computation.13 | convolution fusion | flops 3076 | bytes 2064 | tf_op jit(solution)/shard_map/dot_general | solution.py:24
  1.6 1.1 %bitcast_select_fusion.2 = bf16[256,512]{1,0:T(8,128)(2,1)S(1)} fusion(bf16[1,256,512]{2,1,0:T(8,128)(2,1)} %param.6, pred[256]{0:T(512)(128)(4,1)S(1)} %broadcast_compare_fusion), kind=kLoop, calls=%fused_computation.11 | loop fusion | flops 131072 | bytes 524544 | tf_op jit(solution)/shard_map/jit(_where)/select_n | solution.py:28
  2.6 3.0 %collective-permute-start.1 = (bf16[256,512]{1,0:T(8,128)(2,1)S(1)}, bf16[256,512]{1,0:T(8,128)(2,1)S(1)}, u32[]{:S(2)}, u32[]{:S(2)}) collective-permute-start(bf16[256,512]{1,0:T(8,128)(2,1)S(1)} %bitcast_select_fusion.2), channel_id=1, source_target_pairs={{0,1},{1,2},{2,3},{3,4},{4,5},{5,6},{6,7},{7,0},{8,9},{9,10},{10,1... | collective-permute-start | bytes 786440 | tf_op jit(solution)/shard_map/ppermute | solution.py:34
  5.7 9.3 %collective-permute-done.1 = bf16[256,512]{1,0:T(8,128)(2,1)S(1)} collective-permute-done((bf16[256,512]{1,0:T(8,128)(2,1)S(1)}, bf16[256,512]{1,0:T(8,128)(2,1)S(1)}, u32[]{:S(2)}, u32[]{:S(2)}) %collective-permute-start.1) | collective-permute-done | bytes 262176 | tf_op jit(solution)/shard_map/ppermute | solution.py:34
  15.0 10.2 %collective-permute-done.2 = bf16[256,512]{1,0:T(8,128)(2,1)S(1)} collective-permute-done((bf16[256,512]{1,0:T(8,128)(2,1)S(1)}, bf16[256,512]{1,0:T(8,128)(2,1)S(1)}, u32[]{:S(2)}, u32[]{:S(2)}) %collective-permute-start.2) | collective-permute-done | bytes 262176 | tf_op jit(solution)/shard_map/ppermute | solution.py:34
  25.2 9.3 %collective-permute-done.3 = bf16[256,512]{1,0:T(8,128)(2,1)S(1)} collective-permute-done((bf16[256,512]{1,0:T(8,128)(2,1)S(1)}, bf16[256,512]{1,0:T(8,128)(2,1)S(1)}, u32[]{:S(2)}, u32[]{:S(2)}) %collective-permute-start.3) | collective-permute-done | bytes 262176 | tf_op jit(solution)/shard_map/ppermute | solution.py:34
  34.5 9.1 %collective-permute-done.4 = bf16[256,512]{1,0:T(8,128)(2,1)S(1)} collective-permute-done((bf16[256,512]{1,0:T(8,128)(2,1)S(1)}, bf16[256,512]{1,0:T(8,128)(2,1)S(1)}, u32[]{:S(2)}, u32[]{:S(2)}) %collective-permute-start.4) | collective-permute-done | bytes 262176 | tf_op jit(solution)/shard_map/ppermute | solution.py:34
  43.6 9.1 %collective-permute-done.5 = bf16[256,512]{1,0:T(8,128)(2,1)S(1)} collective-permute-done((bf16[256,512]{1,0:T(8,128)(2,1)S(1)}, bf16[256,512]{1,0:T(8,128)(2,1)S(1)}, u32[]{:S(2)}, u32[]{:S(2)}) %collective-permute-start.5) | collective-permute-done | bytes 262176 | tf_op jit(solution)/shard_map/ppermute | solution.py:34
  52.6 9.7 %collective-permute-done.6 = bf16[256,512]{1,0:T(8,128)(2,1)S(1)} collective-permute-done((bf16[256,512]{1,0:T(8,128)(2,1)S(1)}, bf16[256,512]{1,0:T(8,128)(2,1)S(1)}, u32[]{:S(2)}, u32[]{:S(2)}) %collective-permute-start.6) | collective-permute-done | bytes 262176 | tf_op jit(solution)/shard_map/ppermute | solution.py:34
  62.3 0.7 compare_bitcast_fusion
  63.0 0.1 broadcast_bitcast_fusion
  63.1 8.3 %collective-permute-done.7 = bf16[256,512]{1,0:T(8,128)(2,1)S(1)} collective-permute-done((bf16[256,512]{1,0:T(8,128)(2,1)S(1)}, bf16[256,512]{1,0:T(8,128)(2,1)S(1)}, u32[]{:S(2)}, u32[]{:S(2)}) %collective-permute-start.7) | collective-permute-done | bytes 262176 | tf_op jit(solution)/shard_map/ppermute | solution.py:34
  71.6 0.1 constant_dynamic-update-slice_fusion.8
  71.9 0.0 copy-start.3
  71.9 0.1 constant_dynamic-update-slice_fusion
  72.0 1.9 %copy-done.1 = bf16[4096,512]{1,0:T(8,128)(2,1)} copy-done((bf16[4096,512]{1,0:T(8,128)(2,1)}, bf16[4096,512]{1,0:T(8,128)(2,1)S(1)}, u32[]{:S(2)}) %copy-start.1) | copy-done | bytes 4194328
  74.0 0.7 fusion.7
  74.7 0.0 copy-start.2
  74.7 0.1 copy.11
  74.9 10.6 %all_to_all.19 = bf16[8,64,256]{2,1,0:T(8,128)(2,1)S(1)} all-to-all(bf16[8,64,256]{2,1,0:T(8,128)(2,1)S(1)} %bitcast.38), channel_id=1, replica_groups=mesh['leaf'=4,'grid'=8] {'grid'}, dimensions={0} | all-to-all | bytes 524288 | tf_op jit(solution)/shard_map/all_to_all | solution.py:40
  85.5 0.2 copy.12
  85.7 0.8 broadcast_in_dim.31
  86.5 2.7 %fusion.13 = f32[1,64,512]{2,1,0:T(8,128)} fusion(bf16[64,2048]{1,0:T(8,128)(2,1)S(1)} %bitcast.39, bf16[4096,512]{1,0:T(8,128)(2,1)} %copy-done.1, s32[]{:T(128)S(6)} %select_n.34, f32[1,64,512]{2,1,0:T(8,128)S(1)} %copy-done.3), kind=kOutput, calls=%fused_computation.7 | convolution fusion | flops 134250496 | bytes 2621444 | tf_op jit(solution)/shard_map/dot_general | solution.py:41
  (32 shorter events, 0.3 us)
Async XLA Ops:
  0.6 70.9 %copy-start = (bf16[1,256,512]{2,1,0:T(8,128)(2,1)S(1)}, bf16[1,256,512]{2,1,0:T(8,128)(2,1)}, u32[]{:S(2)}) copy-start(bf16[1,256,512]{2,1,0:T(8,128)(2,1)} %param.6) | copy-start | bytes 786436
  2.6 12.4 %collective-permute-start.1 = (bf16[256,512]{1,0:T(8,128)(2,1)S(1)}, bf16[256,512]{1,0:T(8,128)(2,1)S(1)}, u32[]{:S(2)}, u32[]{:S(2)}) collective-permute-start(bf16[256,512]{1,0:T(8,128)(2,1)S(1)} %bitcast_select_fusion.2), channel_id=1, source_target_pairs={{0,1},{1,2},{2,3},{3,4},{4,5},{5,6},{6,7},{7,0},{8,9},{9,10},{10,1... | collective-permute-start | bytes 786440 | tf_op jit(solution)/shard_map/ppermute | solution.py:34
  15.0 10.2 %collective-permute-start.2 = (bf16[256,512]{1,0:T(8,128)(2,1)S(1)}, bf16[256,512]{1,0:T(8,128)(2,1)S(1)}, u32[]{:S(2)}, u32[]{:S(2)}) collective-permute-start(bf16[256,512]{1,0:T(8,128)(2,1)S(1)} %collective-permute-done.1), channel_id=1, source_target_pairs={{0,1},{1,2},{2,3},{3,4},{4,5},{5,6},{6,7},{7,0},{8,9},{9,10},{10,1... | collective-permute-start | bytes 786440 | tf_op jit(solution)/shard_map/ppermute | solution.py:34
  25.2 9.3 %collective-permute-start.3 = (bf16[256,512]{1,0:T(8,128)(2,1)S(1)}, bf16[256,512]{1,0:T(8,128)(2,1)S(1)}, u32[]{:S(2)}, u32[]{:S(2)}) collective-permute-start(bf16[256,512]{1,0:T(8,128)(2,1)S(1)} %collective-permute-done.2), channel_id=1, source_target_pairs={{0,1},{1,2},{2,3},{3,4},{4,5},{5,6},{6,7},{7,0},{8,9},{9,10},{10,1... | collective-permute-start | bytes 786440 | tf_op jit(solution)/shard_map/ppermute | solution.py:34
  34.5 9.1 %collective-permute-start.4 = (bf16[256,512]{1,0:T(8,128)(2,1)S(1)}, bf16[256,512]{1,0:T(8,128)(2,1)S(1)}, u32[]{:S(2)}, u32[]{:S(2)}) collective-permute-start(bf16[256,512]{1,0:T(8,128)(2,1)S(1)} %collective-permute-done.3), channel_id=1, source_target_pairs={{0,1},{1,2},{2,3},{3,4},{4,5},{5,6},{6,7},{7,0},{8,9},{9,10},{10,1... | collective-permute-start | bytes 786440 | tf_op jit(solution)/shard_map/ppermute | solution.py:34
  43.6 9.1 %collective-permute-start.5 = (bf16[256,512]{1,0:T(8,128)(2,1)S(1)}, bf16[256,512]{1,0:T(8,128)(2,1)S(1)}, u32[]{:S(2)}, u32[]{:S(2)}) collective-permute-start(bf16[256,512]{1,0:T(8,128)(2,1)S(1)} %collective-permute-done.4), channel_id=1, source_target_pairs={{0,1},{1,2},{2,3},{3,4},{4,5},{5,6},{6,7},{7,0},{8,9},{9,10},{10,1... | collective-permute-start | bytes 786440 | tf_op jit(solution)/shard_map/ppermute | solution.py:34
  52.6 9.7 %collective-permute-start.6 = (bf16[256,512]{1,0:T(8,128)(2,1)S(1)}, bf16[256,512]{1,0:T(8,128)(2,1)S(1)}, u32[]{:S(2)}, u32[]{:S(2)}) collective-permute-start(bf16[256,512]{1,0:T(8,128)(2,1)S(1)} %collective-permute-done.5), channel_id=1, source_target_pairs={{0,1},{1,2},{2,3},{3,4},{4,5},{5,6},{6,7},{7,0},{8,9},{9,10},{10,1... | collective-permute-start | bytes 786440 | tf_op jit(solution)/shard_map/ppermute | solution.py:34
  52.6 19.4 %collective-permute-start = (bf16[1,256,2048]{2,1,0:T(8,128)(2,1)}, bf16[1,256,2048]{2,1,0:T(8,128)(2,1)S(1)}, u32[]{:S(2)}, u32[]{:S(2)}) collective-permute-start(bf16[1,256,2048]{2,1,0:T(8,128)(2,1)} %param.5), channel_id=1, source_target_pairs={{0,8},{8,0},{16,24},{24,16},{1,9},{9,1},{17,25},{25,17},{2,10},{10... | collective-permute-start | bytes 3145736 | tf_op jit(solution)/shard_map/ppermute | solution.py:10
  62.3 9.1 %collective-permute-start.7 = (bf16[256,512]{1,0:T(8,128)(2,1)S(1)}, bf16[256,512]{1,0:T(8,128)(2,1)S(1)}, u32[]{:S(2)}, u32[]{:S(2)}) collective-permute-start(bf16[256,512]{1,0:T(8,128)(2,1)S(1)} %collective-permute-done.6), channel_id=1, source_target_pairs={{0,1},{1,2},{2,3},{3,4},{4,5},{5,6},{6,7},{7,0},{8,9},{9,10},{10,1... | collective-permute-start | bytes 786440 | tf_op jit(solution)/shard_map/ppermute | solution.py:34
  63.1 10.9 %copy-start.4 = (bf16[1,256,2048]{2,1,0:T(8,128)(2,1)S(1)}, bf16[1,256,2048]{2,1,0:T(8,128)(2,1)}, u32[]{:S(2)}) copy-start(bf16[1,256,2048]{2,1,0:T(8,128)(2,1)} %param.5) | copy-start | bytes 3145732
  71.9 14.6 %copy-start.3 = (f32[1,64,512]{2,1,0:T(8,128)S(1)}, f32[1,64,512]{2,1,0:T(8,128)}, u32[]{:S(2)}) copy-start(f32[1,64,512]{2,1,0:T(8,128)} %param.9) | copy-start | bytes 393220
  72.0 2.0 %copy-start.1 = (bf16[4096,512]{1,0:T(8,128)(2,1)}, bf16[4096,512]{1,0:T(8,128)(2,1)S(1)}, u32[]{:S(2)}) copy-start(bf16[4096,512]{1,0:T(8,128)(2,1)S(1)} %constant_dynamic-update-slice_fusion) | copy-start | bytes 12582916
  74.7 14.5 %copy-start.2 = (bf16[256,512]{1,0:T(8,128)(2,1)}, bf16[256,512]{1,0:T(8,128)(2,1)S(1)}, u32[]{:S(2)}) copy-start(bf16[256,512]{1,0:T(8,128)(2,1)S(1)} %fusion.7) | copy-start | bytes 786436
